TPU v7x, 32 devices: a whole 2x2x4 slice. The times are simulated.
32 devices in a mesh: pair: 4 (over x, core), dp: 8 (over z, y).
Axes of the slice: x: 2, y: 2, z: 4, core: 2. Of those that a mesh axis runs over, the one named last changes fastest.
Arguments:
- master: float32 [4, 131072], P('pair', 'dp'), may hold values from -6 to 6
- moment1: float32 [4, 131072], P('pair', 'dp'), may hold values from -4 to 4
- moment2: float32 [4, 131072], P('pair', 'dp'), may hold values from 0.05 to 2
- local_grad: bfloat16 [4, 8, 131072], P('pair', 'dp'), may hold values from -6 to 6
- partner: int32 [8, 4], P('dp'), may hold values from 0 to 3, as said below
Outputs:
- new_master: float32 [4, 8, 2, 16384], P('pair', 'dp')
- new_moment1: float32 [4, 8, 2, 16384], P('pair', 'dp')
- new_moment2: float32 [4, 8, 2, 16384], P('pair', 'dp')
Inputs may be any that keep to these rules, and one draw needn't show every extreme that they name: partner[d, partner[d, i]] == i and partner[d, i] != i for every d and i: each row a perfect matching of the 4 pair indices.
All inputs are finite; a program needn't handle non-finite values.
Results may differ from a plain program's by a relative error of at most 0.0003.
Values sent between devices are 32-bit elements; how exact they have to be, the bound alone decides.
A program may use at most 64 MiB of HBM per device.

v0:
```python
import jax
import jax.numpy as jnp
from jax import lax
from jax.sharding import PartitionSpec as P

beta_one = 0.9
beta_two = 0.95
bias_one = 1.0 - 0.9**10
bias_two = 1.0 - 0.95**10
rate = 0.001
decay = 0.1
eps_value = 1e-08


def adamw_update(weights, first, second, grads, scale):
    scaled = scale * grads
    first_new = beta_one * first + (1.0 - beta_one) * scaled
    second_new = beta_two * second + (1.0 - beta_two) * scaled * scaled
    change = first_new / bias_one / (jnp.sqrt(second_new / bias_two) + eps_value) + decay * weights
    return (weights - rate * change, first_new, second_new)


def on_device(master, moment1, moment2, local_grad, partner):
    mine = lax.axis_index("pair")
    mate = partner[0, mine]
    survive = mine < mate
    n_pair = lax.axis_size("pair")
    n_dp = lax.axis_size("dp")
    shard = master.shape[1]
    count = n_pair * n_dp * shard
    term = local_grad[0, 0].astype(jnp.float32).reshape(n_dp, shard)
    reduced = lax.psum_scatter(term, "dp", scatter_dimension=0, tiled=True)[0]
    packed = jnp.stack([master[0], moment1[0], moment2[0], reduced])
    whole = lax.all_gather(packed[None], "pair", axis=0, tiled=True)
    theirs = lax.dynamic_index_in_dim(whole, mate, 0, keepdims=False)
    grads_all = whole[:, 3]
    norm2 = lax.psum(jnp.sum(grads_all * grads_all), "dp")
    scale = 1.0 / jnp.maximum(jnp.sqrt(norm2 / count), 1.0)
    weights = jnp.stack([packed[0], theirs[0]])
    first = jnp.stack([packed[1], theirs[1]])
    second = jnp.stack([packed[2], theirs[2]])
    grads = jnp.stack([reduced, theirs[3]])
    results = adamw_update(weights, first, second, grads, scale)
    return tuple((jnp.where(survive, item, 0.0).reshape(1, 1, 2, shard) for item in results))


def solution(mesh):
    return jax.shard_map(
        on_device,
        mesh=mesh,
        in_specs=(
            P("pair", "dp"),
            P("pair", "dp"),
            P("pair", "dp"),
            P("pair", "dp", None),
            P("dp", None),
        ),
        out_specs=(
            P("pair", "dp", None, None),
            P("pair", "dp", None, None),
            P("pair", "dp", None, None),
        ),
        check_vma=False,
    )
```

profile of v0, /device:TPU:0, one launch (start us, length us, event | category | flops | bytes accessed | tf_op | source)
XLA Modules:
  0.0 143.3 jit_solution(16356764267667255549)
XLA Ops:
  7.2 0.0 copy-start
  7.2 0.0 all-reduce.3.cloned.1.call-start
  7.2 2.6 %convert_reduce_fusion = f32[131072]{0:T(1024)S(1)} fusion(bf16[1,1,131072]{2,1,0:T(2,128)(2,1)} %param.8), kind=kLoop, calls=%fused_computation | loop fusion | flops 131072 | bytes 786432 | tf_op jit(solution)/shard_map/convert_element_type | solution.py:31
  9.8 0.9 reshape.258
  10.7 0.0 copy-start.3
  10.7 0.0 all-reduce.3.cloned.1.call-update
  10.7 0.0 all-gather.4.cloned.1.call-start
  10.8 0.0 copy-start.4
  10.8 0.6 copy-done.4
  11.4 0.6 dynamic-slice.1
  12.0 74.9 %all-reduce.3.cloned.1.call-done = f32[8,16384]{1,0:T(8,128)} async-done(((f32[8,16384]{1,0:T(8,128)}), f32[8,16384]{1,0:T(8,128)}) %all-reduce.3.cloned.1.call-update) | async-done | bytes 524304
  86.9 0.0 copy-start.1
  86.9 0.0 copy-start.2
  86.9 1.8 %constant_dynamic-slice_fusion.1 = f32[1,16384]{1,0:T(1,128)S(1)} fusion(f32[8,16384]{1,0:T(8,128)} %all-reduce.3.cloned.1.call-done, u32[]{:T(128)} %bitcast.2), kind=kLoop, calls=%fused_computation.19 | loop fusion | bytes 131076
  88.7 0.0 copy-done.3
  88.7 0.0 copy-done.1
  88.7 0.0 copy-done.2
  88.7 1.0 maximum_bitcast_fusion
  89.7 0.0 all-gather.4.cloned.1.call-update
  89.7 0.0 copy-done
  89.7 0.6 constant_dynamic-slice_fusion
  92.9 12.8 %all-gather.4.cloned.1.call-done = f32[4,4,16384]{2,1,0:T(4,128)} async-done(((f32[1,4,16384]{2,1,0:T(4,128)}), f32[4,4,16384]{2,1,0:T(4,128)}) %all-gather.4.cloned.1.call-update) | async-done | bytes 1048592 | tf_op jit(solution)/shard_map/all_gather | solution.py:34
  105.7 2.4 %fusion = f32[]{:T(128)} fusion(f32[4,4,16384]{2,1,0:T(4,128)} %all-gather.4.cloned.1.call-done), kind=kLoop, calls=%fused_computation.3 | loop fusion | flops 131071 | bytes 262148 | tf_op jit(solution)/shard_map/reduce_sum | solution.py:37
  108.1 1.7 %fusion.5 = f32[1,1,1,16384]{3,2,1,0:T(1,128)S(1)} fusion(f32[8,16384]{1,0:T(8,128)} %all-reduce.3.cloned.1.call-done, u32[]{:T(128)} %bitcast.2), kind=kLoop, calls=%fused_computation.20 | loop fusion | bytes 131076 | tf_op jit(solution)/shard_map/stack | solution.py:42
  109.8 22.0 %psum.7 = f32[]{:T(128)} all-reduce(f32[]{:T(128)} %fusion), channel_id=1, replica_groups=mesh['pair'=4,'dp'=8] {'dp'}, use_global_device_ids=true, to_apply=%region_2.3 | all-reduce | flops 1 | bytes 8 | tf_op jit(solution)/shard_map/psum | solution.py:37
  132.6 1.6 %dynamic-slice_bitcast_fusion.2 = (f32[1,1,1,16384]{3,2,1,0:T(1,128)S(1)}, f32[1,1,1,16384]{3,2,1,0:T(1,128)S(1)}, f32[1,1,1,16384]{3,2,1,0:T(1,128)S(1)}, f32[1,1,1,16384]{3,2,1,0:T(1,128)S(1)}) fusion(f32[4,4,16384]{2,1,0:T(4,128)} %all-gather.4.cloned.1.call-done, s32[]{:T(128)S(6)} %select_n.46, s32[]{:T(128)S(6)} %add.73, s32[]{:T(128)S(6)} %add.74, ...), kind=kLoop, calls=%fused_computation.16 | loop fusion | bytes 524304 | tf_op jit(solution)/shard_map/stack | solution.py:40
  134.2 1.2 broadcast_select_fusion.1
  135.4 1.0 subtract_select_fusion
Async XLA Ops:
  7.2 82.5 %copy-start = (s32[1,4]{1,0:T(1,128)S(1)}, s32[1,4]{1,0:T(1,128)}, u32[]{:S(2)}) copy-start(s32[1,4]{1,0:T(1,128)} %param.9) | copy-start | bytes 52
  7.2 79.7 %all-reduce.3.cloned.1.call-start = ((), (), s32[]{:S(2)}) async-start(), calls=%async_computation.1 | async-start | bytes 1048576
  10.7 78.0 %copy-start.3 = (f32[1,16384]{1,0:T(1,128)S(1)}, f32[1,16384]{1,0:T(1,128)}, u32[]{:S(2)}) copy-start(f32[1,16384]{1,0:T(1,128)} %param.5) | copy-start | bytes 196612
  10.7 95.0 %all-gather.4.cloned.1.call-start = ((), (), s32[]{:S(2)}) async-start(), calls=%async_computation | async-start | bytes 1310720 | tf_op jit(solution)/shard_map/all_gather | solution.py:34
  10.8 0.7 copy-start.4
  86.9 1.8 %copy-start.1 = (f32[1,16384]{1,0:T(1,128)S(1)}, f32[1,16384]{1,0:T(1,128)}, u32[]{:S(2)}) copy-start(f32[1,16384]{1,0:T(1,128)} %param.7) | copy-start | bytes 196612
  86.9 1.8 %copy-start.2 = (f32[1,16384]{1,0:T(1,128)S(1)}, f32[1,16384]{1,0:T(1,128)}, u32[]{:S(2)}) copy-start(f32[1,16384]{1,0:T(1,128)} %param.6) | copy-start | bytes 196612
Sparse Core Ops, SparseCore 0:
  11.4 75.4 all-reduce.2
  89.8 15.8 all-gather.3
where the time goes:
time: 144 us; the launch traced here: 143 us
  waiting for transfers between devices  87.8 us (61%)
  blocking collectives  22 us (15%)
  between operations  17.4 us (12%)
  other arithmetic  8.12 us (6%)
  local copies, waits for them, and re-layouts  7.83 us (5%)
    unnamed x3, waiting for transfers between devices  75 us
    psum x1, blocking collectives, on_device(): norm2 = lax.psum(jnp.sum(grads_all * grads_all), 'dp')  22 us
    all_gather x1, waiting for transfers between devices, on_device(): whole = lax.all_gather(packed[None], 'pair', axis=0, tiled=True)  12.8 us
    unnamed x12, local copies, waits for them, and re-layouts  3.02 us
  transfers between devices with their start and end apart: 2, of which 2 were waited for; matrix products, arithmetic and copies ran while one was open for 1% of the time, Pallas kernels for 0%

commit v1 on v0

v1 whole, which is shorter than its diff:
```python
import functools

import jax
import jax.numpy as jnp
from jax import lax
from jax.experimental import pallas as pl
from jax.experimental.pallas import tpu as pltpu
from jax.sharding import PartitionSpec as P

MESH = pl.DeviceIdType.MESH
LANES = 128

beta_one = 0.9
beta_two = 0.95
bias_one = 1.0 - 0.9**10
bias_two = 1.0 - 0.95**10
rate = 0.001
decay = 0.1
eps_value = 1e-08


def adamw_update(weights, first, second, grads, scale):
    scaled = scale * grads
    first_new = beta_one * first + (1.0 - beta_one) * scaled
    second_new = beta_two * second + (1.0 - beta_two) * scaled * scaled
    change = first_new / bias_one / (jnp.sqrt(second_new / bias_two) + eps_value) + decay * weights
    return (weights - rate * change, first_new, second_new)


def near_split(n):
    inner = 1
    while n % (inner * 2) == 0 and (inner * 2) ** 2 <= n:
        inner *= 2
    return n // inner, inner


def remote(src, dst, send_sem, recv_sem, **where):
    return pltpu.make_async_remote_copy(
        src_ref=src,
        dst_ref=dst,
        send_sem=send_sem,
        recv_sem=recv_sem,
        device_id=where,
        device_id_type=MESH,
    )


def kernel(
    n_pair,
    n_dp,
    partner,
    master,
    moment1,
    moment2,
    grad,
    out_w,
    out_m,
    out_v,
    own,
    theirs,
    near,
    partial,
    far,
    total,
    theirs_total,
    norm_pair,
    norm_pair_in,
    norm_dp,
    norm_dp_in,
    own_sem,
    state_send,
    state_recv,
    near_send,
    near_recv,
    far_send,
    far_recv,
    total_send,
    total_recv,
    pair_send,
    pair_recv,
    dp_send,
    dp_recv,
):
    outer, inner = near_split(n_dp)
    mine = lax.axis_index("pair")
    me = lax.axis_index("dp")
    a, b = lax.div(me, inner), lax.rem(me, inner)
    rows = master.shape[0]
    order = sorted(range(1, outer), key=lambda k: abs(2 * k - outer)) + [0]

    barrier = pltpu.get_barrier_semaphore()
    for k in range(1, n_dp):
        pl.semaphore_signal(barrier, inc=1, device_id={"dp": lax.rem(me + k, n_dp)}, device_id_type=MESH)
    for k in range(1, n_pair):
        pl.semaphore_signal(barrier, inc=1, device_id={"pair": lax.rem(mine + k, n_pair)}, device_id_type=MESH)

    states = (master, moment1, moment2)
    loads = [pltpu.make_async_copy(ref, own.at[i], own_sem.at[i]) for i, ref in enumerate(states)]
    for load in loads:
        load.start()
    pl.semaphore_wait(barrier, n_dp + n_pair - 2)

    def near_copy(j, k):
        to = a * inner + lax.rem(b + j, inner)
        block = lax.rem(a + k, outer) * inner + lax.rem(b + j, inner)
        return remote(grad.at[block], near.at[j - 1, k], near_send.at[j - 1, k], near_recv.at[j - 1, k], dp=to)

    for k in order:
        for j in range(1, inner):
            near_copy(j, k).start()

    def state_copy(q, i):
        return remote(states[i], theirs.at[mine, i], state_send.at[q, i], state_recv.at[mine, i], pair=q)

    def state_arrival(s, i):
        return remote(states[i], theirs.at[s, i], state_send.at[0, i], state_recv.at[s, i], pair=s)

    for q in range(n_pair - 1):

        @pl.when(q < mine)
        def _():
            for i in range(3):
                state_copy(q, i).start()

    def far_copy(k):
        to = lax.rem(a + k, outer) * inner + b
        return remote(partial.at[k - 1], far.at[k - 1], far_send.at[k - 1], far_recv.at[k - 1], dp=to)

    def level_one(k):
        for j in range(1, inner):
            near_copy(j, k).wait_recv()
        acc = grad[lax.rem(a + k, outer) * inner + b]
        for j in range(1, inner):
            acc = acc + near[j - 1, k]
        return acc

    for k in order[:-1]:
        partial[k - 1] = level_one(k)
        far_copy(k).start()
    acc = level_one(0)
    for k in order[:-1]:
        far_copy(k).wait_recv()
        acc = acc + far[k - 1]
    total[...] = acc

    def tile_sum(x):
        return jnp.sum(x.reshape(rows // 8, 8, LANES), axis=0)

    norm_pair[...] = tile_sum(acc * acc)

    def pair_copy(k):
        to = lax.rem(mine + k, n_pair)
        return remote(norm_pair, norm_pair_in.at[k - 1], pair_send.at[k - 1], pair_recv.at[k - 1], pair=to)

    for k in range(1, n_pair):
        pair_copy(k).start()

    def total_copy(q):
        return remote(total, theirs_total.at[mine], total_send.at[q], total_recv.at[mine], pair=q)

    def total_arrival(s):
        return remote(total, theirs_total.at[s], total_send.at[0], total_recv.at[s], pair=s)

    for q in range(n_pair - 1):

        @pl.when(q < mine)
        def _():
            total_copy(q).start()

    norm = norm_pair[...]
    for k in range(1, n_pair):
        pair_copy(k).wait_recv()
        norm = norm + norm_pair_in[k - 1]
    norm_dp[...] = norm

    def dp_copy(k):
        to = lax.rem(me + k, n_dp)
        return remote(norm_dp, norm_dp_in.at[k - 1], dp_send.at[k - 1], dp_recv.at[k - 1], dp=to)

    for k in range(1, n_dp):
        dp_copy(k).start()

    for load in loads:
        load.wait()
    for s in range(1, n_pair):

        @pl.when(s > mine)
        def _():
            for i in range(3):
                state_arrival(s, i).wait_recv()
            total_arrival(s).wait_recv()

    for k in range(1, n_dp):
        dp_copy(k).wait_recv()
        norm = norm + norm_dp_in[k - 1]

    norm2 = jnp.sum(norm, keepdims=True)
    count = n_pair * n_dp * rows * LANES
    scale = 1.0 / jnp.maximum(jnp.sqrt(norm2 / count), 1.0)

    mate = partner[0, mine]
    survive = mate > mine
    outs = (out_w, out_m, out_v)
    for slot in range(2):
        if slot == 0:
            args = (own[0], own[1], own[2], total[...])
        else:
            args = (theirs[mate, 0], theirs[mate, 1], theirs[mate, 2], theirs_total[mate])
        for out, value in zip(outs, adamw_update(*args, scale)):
            out[pl.ds(slot, rows, stride=2), :] = jnp.where(survive, value, 0.0)

    for k in order:
        for j in range(1, inner):
            near_copy(j, k).wait_send()
    for k in order[:-1]:
        far_copy(k).wait_send()
    for k in range(1, n_pair):
        pair_copy(k).wait_send()
    for k in range(1, n_dp):
        dp_copy(k).wait_send()
    for q in range(n_pair - 1):

        @pl.when(q < mine)
        def _():
            for i in range(3):
                state_copy(q, i).wait_send()
            total_copy(q).wait_send()


def on_device(n_pair, n_dp, master, moment1, moment2, local_grad, partner):
    shard = master.shape[1]
    rows = shard // LANES
    outer, inner = near_split(n_dp)
    grad = local_grad.astype(jnp.float32).reshape(n_dp, rows, LANES)
    f32 = jnp.float32
    vmem, smem, hbm = pltpu.VMEM, pltpu.SMEM, pl.ANY
    dma = pltpu.SemaphoreType.DMA
    block = (rows, LANES)
    tile = (8, LANES)
    levels = max(outer - 1, 1)
    results = pl.pallas_call(
        functools.partial(kernel, n_pair, n_dp),
        out_shape=[jax.ShapeDtypeStruct((2 * rows, LANES), f32)] * 3,
        in_specs=[pl.BlockSpec(memory_space=smem)]
        + [pl.BlockSpec(memory_space=hbm)] * 3
        + [pl.BlockSpec(memory_space=vmem)],
        out_specs=[pl.BlockSpec(memory_space=vmem)] * 3,
        scratch_shapes=[
            vmem((3, *block), f32),
            vmem((n_pair, 3, *block), f32),
            vmem((max(inner - 1, 1), outer, *block), f32),
            vmem((levels, *block), f32),
            vmem((levels, *block), f32),
            vmem(block, f32),
            vmem((n_pair, *block), f32),
            vmem(tile, f32),
            vmem((n_pair - 1, *tile), f32),
            vmem(tile, f32),
            vmem((n_dp - 1, *tile), f32),
            dma((3,)),
            dma((n_pair, 3)),
            dma((n_pair, 3)),
            dma((max(inner - 1, 1), outer)),
            dma((max(inner - 1, 1), outer)),
            dma((levels,)),
            dma((levels,)),
            dma((n_pair,)),
            dma((n_pair,)),
            dma((n_pair - 1,)),
            dma((n_pair - 1,)),
            dma((n_dp - 1,)),
            dma((n_dp - 1,)),
        ],
        compiler_params=pltpu.CompilerParams(collective_id=0, has_side_effects=True),
    )(
        partner,
        master.reshape(block),
        moment1.reshape(block),
        moment2.reshape(block),
        grad,
    )
    return tuple(
        item.reshape(rows, 2, LANES).transpose(1, 0, 2).reshape(1, 1, 2, shard) for item in results
    )


def solution(mesh):
    n_pair, n_dp = mesh.shape["pair"], mesh.shape["dp"]
    return jax.shard_map(
        functools.partial(on_device, n_pair, n_dp),
        mesh=mesh,
        in_specs=(
            P("pair", "dp"),
            P("pair", "dp"),
            P("pair", "dp"),
            P("pair", "dp", None),
            P("dp", None),
        ),
        out_specs=(
            P("pair", "dp", None, None),
            P("pair", "dp", None, None),
            P("pair", "dp", None, None),
        ),
        check_vma=False,
    )
```

time: 144 us -> 32.8 us (0.23)
  waiting for transfers between devices: 87.8 us -> 0 us
  Pallas kernels: 0 us -> 26.3 us
  blocking collectives: 22 us -> 0 us
  between operations: 17.4 us -> 0.65 us
  other arithmetic: 8.12 us -> 2.37 us
  local copies, waits for them, and re-layouts: 7.83 us -> 3.21 us
    unnamed x3 -> x0, waiting for transfers between devices: 75 us -> none
    pallas_call x0 -> x1, Pallas kernels: none -> 26.3 us  [on_device(): pl.pallas_call(functools.partial(kernel, n_pair, n_dp), out_shape=[jax.Sh...]
    psum x1 -> x0, blocking collectives: 22 us -> none  [on_device(): norm2 = lax.psum(jnp.sum(grads_all * grads_all), 'dp')]
    all_gather x1 -> x0, waiting for transfers between devices: 12.8 us -> none  [on_device(): whole = lax.all_gather(packed[None], 'pair', axis=0, tiled=True)]
    another operation x2 -> x0, local copies, waits for them, and re-layouts: 3.35 us -> none  [the longest x1 1.73 us: on_device(): grads = jnp.stack([reduced, theirs[3]])]
    convert_element_type x1 -> x0, other arithmetic: 2.56 us -> none  [on_device(): term = local_grad[0, 0].astype(jnp.float32).reshape(n_dp, shard)]
    reshape x0 -> x1, other arithmetic: none -> 2.37 us  [on_device(): grad = local_grad.astype(jnp.float32).reshape(n_dp, rows, LANES)]
    reduce_sum x1 -> x0, other arithmetic: 2.37 us -> none  [on_device(): norm2 = lax.psum(jnp.sum(grads_all * grads_all), 'dp')]
  transfers between devices with their start and end apart: 2 -> 0, of which waited for: 2 -> 0; matrix products, arithmetic and copies ran while one was open for 1% -> 0% of each run, Pallas kernels for 0% -> 0%
where the time goes in v1:
time: 32.8 us; the launch traced here: 32.5 us
  Pallas kernels  26.3 us (80%)
  local copies, waits for them, and re-layouts  3.21 us (10%)
  other arithmetic  2.37 us (7%)
  between operations  0.65 us (2%)
    pallas_call x1, Pallas kernels, on_device(): pl.pallas_call(functools.partial(kernel, n_pair, n_dp), out_shape=[jax.Sh...  26.3 us
    unnamed x7, local copies, waits for them, and re-layouts  3.21 us
    reshape x1, other arithmetic, on_device(): grad = local_grad.astype(jnp.float32).reshape(n_dp, rows, LANES)  2.37 us

profile of v1, /device:TPU:0, one launch (start us, length us, event | category | flops | bytes accessed | tf_op | source)
XLA Modules:
  0.0 32.5 jit_solution(2293625582325590469)
XLA Ops:
  0.6 2.4 %reshape.49 = f32[1,1,131072]{2,1,0:T(1,128)} convert(bf16[1,1,131072]{2,1,0:T(2,128)(2,1)} %param.8) | non-fusion elementwise | flops 131072 | bytes 786432 | tf_op jit(solution)/shard_map/reshape | solution.py:234
  3.0 26.3 %shard_map.76 = (f32[256,128]{1,0:T(8,128)}, f32[256,128]{1,0:T(8,128)}, f32[256,128]{1,0:T(8,128)}) custom-call(s32[1,4]{1,0:T(1,128)} %partner.1, f32[128,128]{1,0:T(8,128)} %bitcast.23, f32[128,128]{1,0:T(8,128)} %bitcast.24, f32[128,128]{1,0:T(8,128)} %bitcast.25, f32[8,128,128]{2,1,0:T(8,128)} %bitcast.19), custom_call_target="tpu_custom_call" | custom-call | tf_op jit(solution)/shard_map/pallas_call | solution.py:241
  29.3 0.0 copy-start.1
  29.3 1.6 %copy.14 = f32[1,1,2,16384]{3,2,1,0:T(2,128)} copy(f32[1,1,2,16384]{3,2,1,0:T(2,128)} %bitcast.22) | data formatting | bytes 262144
  30.9 0.0 copy-done.1
  30.9 0.0 copy-start
  30.9 0.7 %copy.15 = f32[1,1,2,16384]{3,2,1,0:T(2,128)} copy(f32[1,1,2,16384]{3,2,1,0:T(2,128)S(1)} %bitcast.21) | data formatting | bytes 262144
  31.6 0.3 copy-done
  31.9 0.7 %copy.16 = f32[1,1,2,16384]{3,2,1,0:T(2,128)} copy(f32[1,1,2,16384]{3,2,1,0:T(2,128)S(1)} %bitcast.20) | data formatting | bytes 262144
Async XLA Ops:
  29.3 1.6 %copy-start.1 = (f32[256,128]{1,0:T(8,128)S(1)}, f32[256,128]{1,0:T(8,128)}, u32[]{:S(2)}) copy-start(f32[256,128]{1,0:T(8,128)} %get-tuple-element.7) | copy-start | bytes 393220
  30.9 1.0 %copy-start = (f32[256,128]{1,0:T(8,128)S(1)}, f32[256,128]{1,0:T(8,128)}, u32[]{:S(2)}) copy-start(f32[256,128]{1,0:T(8,128)} %get-tuple-element.8) | copy-start | bytes 393220

commit v2 on v1

v2 whole, which is shorter than its diff:
```python
import functools

import jax
import jax.numpy as jnp
from jax import lax
from jax.experimental import pallas as pl
from jax.experimental.pallas import tpu as pltpu
from jax.sharding import PartitionSpec as P

MESH = pl.DeviceIdType.MESH
LANES = 128
PARTS = 2

beta_one = 0.9
beta_two = 0.95
bias_one = 1.0 - 0.9**10
bias_two = 1.0 - 0.95**10
rate = 0.001
decay = 0.1
eps_value = 1e-08


def adamw_update(weights, first, second, grads, scale):
    scaled = scale * grads
    first_new = beta_one * first + (1.0 - beta_one) * scaled
    second_new = beta_two * second + (1.0 - beta_two) * scaled * scaled
    change = first_new / bias_one / (jnp.sqrt(second_new / bias_two) + eps_value) + decay * weights
    return (weights - rate * change, first_new, second_new)


def near_split(n):
    inner = 1
    while n % (inner * 2) == 0 and (inner * 2) ** 2 <= n:
        inner *= 2
    return n // inner, inner


def remote(src, dst, send_sem, recv_sem, **where):
    return pltpu.make_async_remote_copy(
        src_ref=src,
        dst_ref=dst,
        send_sem=send_sem,
        recv_sem=recv_sem,
        device_id=where,
        device_id_type=MESH,
    )


def kernel(
    n_pair,
    n_dp,
    partner,
    master,
    moment1,
    moment2,
    local_grad,
    out_w,
    out_m,
    out_v,
    raw,
    grad,
    own,
    theirs,
    near,
    partial,
    far,
    total,
    theirs_total,
    norm_dp,
    norm_in,
    own_sem,
    state_send,
    state_recv,
    near_send,
    near_recv,
    far_send,
    far_recv,
    total_send,
    total_recv,
    norm_send,
    norm_recv,
    raw_sem,
    up_sem,
    down_sem,
):
    outer, inner = near_split(n_dp)
    mine = lax.axis_index("pair")
    me = lax.axis_index("dp")
    a, b = lax.div(me, inner), lax.rem(me, inner)
    rows = master.shape[0]
    order = sorted(range(1, outer), key=lambda k: abs(2 * k - outer)) + [0]

    barrier = pltpu.get_barrier_semaphore()
    for j in range(1, inner):
        pl.semaphore_signal(barrier, inc=1, device_id={"dp": a * inner + lax.rem(b + j, inner)}, device_id_type=MESH)
    for k in range(1, n_pair):
        pl.semaphore_signal(barrier, inc=1, device_id={"pair": lax.rem(mine + k, n_pair)}, device_id_type=MESH)
    above, below = a < outer - 1, a > 0

    def tell(sems):
        @pl.when(above)
        def _():
            pl.semaphore_signal(sems[0], inc=1, device_id={"dp": me + inner}, device_id_type=MESH)

        @pl.when(below)
        def _():
            pl.semaphore_signal(sems[1], inc=1, device_id={"dp": me - inner}, device_id_type=MESH)

    tell((barrier, barrier))

    states = (master, moment1, moment2)
    loads = [pltpu.make_async_copy(ref, own.at[i], own_sem.at[i]) for i, ref in enumerate(states)]
    shard = rows * LANES

    def piece_of(k):
        first = lax.rem(a + k, outer) * inner
        return pl.ds(pl.multiple_of(first * shard, shard), inner * shard)

    pieces = [pltpu.make_async_copy(local_grad.at[0, :, piece_of(k)], raw.at[:, piece_of(k)], raw_sem.at[k]) for k in range(outer)]
    for k in order:
        pieces[k].start()
    for load in loads:
        load.start()

    def widen(k):
        pieces[k].wait()
        for i in range(inner):
            block = lax.rem(a + k, outer) * inner + i
            line = raw[:, pl.ds(pl.multiple_of(block * shard, shard), shard)]
            grad[block] = line.astype(jnp.float32).reshape(rows, LANES)

    for k in order:
        widen(k)
    pl.semaphore_wait(barrier, inner + n_pair - 2 + above.astype(jnp.int32) + below.astype(jnp.int32))

    part = rows // PARTS
    cuts = [pl.ds(h * part, part) for h in range(PARTS)]

    def near_copy(j, k, h):
        to = a * inner + lax.rem(b + j, inner)
        block = lax.rem(a + k, outer) * inner + lax.rem(b + j, inner)
        sems = near_send.at[j - 1, k, h], near_recv.at[j - 1, k, h]
        return remote(grad.at[block, cuts[h]], near.at[j - 1, k, cuts[h]], *sems, dp=to)

    steps = [(k, h) for k in order[:-1] for h in range(PARTS)]
    last = [(0, h) for h in range(PARTS)]
    for k, h in steps + last:
        for j in range(1, inner):
            near_copy(j, k, h).start()

    def state_copy(q, i):
        return remote(states[i], theirs.at[mine, i], state_send.at[q, i], state_recv.at[mine, i], pair=q)

    def state_arrival(s, i):
        return remote(states[i], theirs.at[s, i], state_send.at[0, i], state_recv.at[s, i], pair=s)

    for q in range(n_pair - 1):

        @pl.when(q < mine)
        def _():
            for i in range(3):
                state_copy(q, i).start()

    for r in range(outer - 2):
        tell((up_sem.at[r], down_sem.at[r]))

        @pl.when(below)
        def _():
            pl.semaphore_wait(up_sem.at[r], 1)

        @pl.when(above)
        def _():
            pl.semaphore_wait(down_sem.at[r], 1)

    def far_copy(k, h):
        to = lax.rem(a + k, outer) * inner + b
        sems = far_send.at[k - 1, h], far_recv.at[k - 1, h]
        return remote(partial.at[k - 1, cuts[h]], far.at[k - 1, cuts[h]], *sems, dp=to)

    def level_one(k, h):
        acc = grad[lax.rem(a + k, outer) * inner + b, cuts[h]]
        for j in range(1, inner):
            near_copy(j, k, h).wait_recv()
            acc = acc + near[j - 1, k, cuts[h]]
        return acc

    for k, h in steps:
        partial[k - 1, cuts[h]] = level_one(k, h)
        far_copy(k, h).start()
    for k, h in last:
        total[cuts[h]] = level_one(k, h)
    for k, h in steps:
        far_copy(k, h).wait_recv()
    acc = total[...]
    for k in order[:-1]:
        acc = acc + far[k - 1]
    total[...] = acc

    norm_dp[...] = jnp.sum(acc * acc, axis=0, keepdims=True)

    def norm_copy(i, k):
        n = i * n_dp + k - 1
        return remote(norm_dp, norm_in.at[pl.ds(n, 1)], norm_send, norm_recv, pair=lax.rem(mine + i, n_pair), dp=lax.rem(me + k, n_dp))

    peers = [(i, k) for k in range(n_dp) for i in range(n_pair) if i + k]
    for i, k in peers:
        norm_copy(i, k).start()

    def total_copy(q):
        return remote(total, theirs_total.at[mine], total_send.at[q], total_recv.at[mine], pair=q)

    def total_arrival(s):
        return remote(total, theirs_total.at[s], total_send.at[0], total_recv.at[s], pair=s)

    for q in range(n_pair - 1):

        @pl.when(q < mine)
        def _():
            total_copy(q).start()

    for load in loads:
        load.wait()
    for s in range(1, n_pair):

        @pl.when(s > mine)
        def _():
            for i in range(3):
                state_arrival(s, i).wait_recv()
            total_arrival(s).wait_recv()

    norm = norm_dp[...]
    pltpu.make_async_copy(norm_in, norm_in, norm_recv).wait()
    norm = norm + jnp.sum(norm_in[...], axis=0, keepdims=True)

    norm2 = jnp.sum(norm, keepdims=True)
    count = n_pair * n_dp * rows * LANES
    scale = 1.0 / jnp.maximum(jnp.sqrt(norm2 / count), 1.0)

    mate = partner[0, mine]
    survive = mate > mine
    outs = (out_w, out_m, out_v)
    for slot in range(2):
        if slot == 0:
            args = (own[0], own[1], own[2], total[...])
        else:
            args = (theirs[mate, 0], theirs[mate, 1], theirs[mate, 2], theirs_total[mate])
        for out, value in zip(outs, adamw_update(*args, scale)):
            out[pl.ds(slot, rows, stride=2), :] = jnp.where(survive, value, 0.0)

    for k, h in steps + last:
        for j in range(1, inner):
            near_copy(j, k, h).wait_send()
    for k, h in steps:
        far_copy(k, h).wait_send()
    pltpu.make_async_copy(norm_in, norm_in, norm_send).wait()
    for q in range(n_pair - 1):

        @pl.when(q < mine)
        def _():
            for i in range(3):
                state_copy(q, i).wait_send()
            total_copy(q).wait_send()


def put_out(in_w, in_m, in_v, out_w, out_m, out_v, sem):
    copies = [
        pltpu.make_async_copy(src, dst, sem.at[i])
        for i, (src, dst) in enumerate(((in_w, out_w), (in_m, out_m), (in_v, out_v)))
    ]
    for copy in copies:
        copy.start()
    for copy in copies:
        copy.wait()


def on_device(n_pair, n_dp, master, moment1, moment2, local_grad, partner):
    shard = master.shape[1]
    rows = shard // LANES
    outer, inner = near_split(n_dp)
    f32 = jnp.float32
    vmem, smem, hbm = pltpu.VMEM, pltpu.SMEM, pl.ANY
    dma = pltpu.SemaphoreType.DMA
    block = (rows, LANES)
    levels = max(outer - 1, 1)
    results = pl.pallas_call(
        functools.partial(kernel, n_pair, n_dp),
        out_shape=[vmem((2 * rows, LANES), f32)] * 3,
        in_specs=[pl.BlockSpec(memory_space=smem)]
        + [pl.BlockSpec(memory_space=hbm)] * 4,
        out_specs=[pl.BlockSpec(memory_space=vmem)] * 3,
        scratch_shapes=[
            vmem((1, n_dp * shard), jnp.bfloat16),
            vmem((n_dp, *block), f32),
            vmem((3, *block), f32),
            vmem((n_pair, 3, *block), f32),
            vmem((max(inner - 1, 1), outer, *block), f32),
            vmem((levels, *block), f32),
            vmem((levels, *block), f32),
            vmem(block, f32),
            vmem((n_pair, *block), f32),
            vmem((1, LANES), f32),
            vmem((n_pair * n_dp - 1, LANES), f32),
            dma((3,)),
            dma((n_pair, 3)),
            dma((n_pair, 3)),
            dma((max(inner - 1, 1), outer, PARTS)),
            dma((max(inner - 1, 1), outer, PARTS)),
            dma((levels, PARTS)),
            dma((levels, PARTS)),
            dma((n_pair,)),
            dma((n_pair,)),
            dma,
            dma,
            dma((outer,)),
            pltpu.SemaphoreType.REGULAR((max(outer - 2, 1),)),
            pltpu.SemaphoreType.REGULAR((max(outer - 2, 1),)),
        ],
        compiler_params=pltpu.CompilerParams(collective_id=0, has_side_effects=True),
    )(
        partner,
        master.reshape(block),
        moment1.reshape(block),
        moment2.reshape(block),
        local_grad,
    )
    results = pl.pallas_call(
        put_out,
        out_shape=[jax.ShapeDtypeStruct((2 * rows, LANES), f32)] * 3,
        in_specs=[pl.BlockSpec(memory_space=vmem)] * 3,
        out_specs=[pl.BlockSpec(memory_space=hbm)] * 3,
        scratch_shapes=[dma((3,))],
    )(*[pltpu.with_memory_space_constraint(item, pltpu.VMEM) for item in results])
    return tuple(
        item.reshape(rows, 2, LANES).transpose(1, 0, 2).reshape(1, 1, 2, shard) for item in results
    )


def solution(mesh):
    n_pair, n_dp = mesh.shape["pair"], mesh.shape["dp"]
    return jax.shard_map(
        functools.partial(on_device, n_pair, n_dp),
        mesh=mesh,
        in_specs=(
            P("pair", "dp"),
            P("pair", "dp"),
            P("pair", "dp"),
            P("pair", "dp", None),
            P("dp", None),
        ),
        out_specs=(
            P("pair", "dp", None, None),
            P("pair", "dp", None, None),
            P("pair", "dp", None, None),
        ),
        check_vma=False,
    )
```

time: 32.8 us -> 21.8 us (0.66)
  Pallas kernels: 26.3 us -> 21 us
  local copies, waits for them, and re-layouts: 3.21 us -> 0 us
  other arithmetic: 2.37 us -> 0 us
    pallas_call x1 -> x2, Pallas kernels: 26.3 us -> 21 us  [the longest x1 20.2 us: on_device(): pl.pallas_call(functools.partial(kernel, n_pair, n_dp), out_shape=[vmem((...]
    unnamed x7 -> x0, local copies, waits for them, and re-layouts: 3.21 us -> none
    reshape x1 -> x0, other arithmetic: 2.37 us -> none  [on_device(): grad = local_grad.astype(jnp.float32).reshape(n_dp, rows, LANES)]
where the time goes in v2:
time: 21.8 us; the launch traced here: 21.7 us
  Pallas kernels  21 us (96%)
  between operations  0.64 us (3%)
    pallas_call x1, Pallas kernels, on_device(): pl.pallas_call(functools.partial(kernel, n_pair, n_dp), out_shape=[vmem((...  20.2 us
    pallas_call x1, Pallas kernels, on_device(): pl.pallas_call(put_out, out_shape=[jax.ShapeDtypeStruct((2 * rows, LANES)...  0.77 us

profile of v2, /device:TPU:0, one launch (start us, length us, event | category | flops | bytes accessed | tf_op | source)
XLA Modules:
  0.0 21.7 jit_solution(7339587285984221533)
XLA Ops:
  0.6 20.2 %shard_map.76 = (f32[256,128]{1,0:T(8,128)S(1)}, f32[256,128]{1,0:T(8,128)S(1)}, f32[256,128]{1,0:T(8,128)S(1)}) custom-call(s32[1,4]{1,0:T(1,128)} %partner.1, f32[128,128]{1,0:T(8,128)} %bitcast.18, f32[128,128]{1,0:T(8,128)} %bitcast.19, f32[128,128]{1,0:T(8,128)} %bitcast.20, bf16[1,1,131072]{2,1,0:T(2,128)(2,1)} %local_grad.1), custom_call_target="tpu_custom_call" | custom-call | tf_op jit(solution)/shard_map/pallas_call | solution.py:285
  20.9 0.8 %shard_map.77 = (f32[256,128]{1,0:T(8,128)}, f32[256,128]{1,0:T(8,128)}, f32[256,128]{1,0:T(8,128)}) custom-call(f32[256,128]{1,0:T(8,128)S(1)} %get-tuple-element.9.in_w, f32[256,128]{1,0:T(8,128)S(1)} %get-tuple-element.10.in_m, f32[256,128]{1,0:T(8,128)S(1)} %get-tuple-element.11.in_v), custom_call_target="tpu_custom_call" | custom-call | tf_op jit(solution)/shard_map/pallas_call | solution.py:326

commit v3 on v2

--- a/solution.py
+++ b/solution.py
@@ -88,7 +88,15 @@
     me = lax.axis_index("dp")
     a, b = lax.div(me, inner), lax.rem(me, inner)
     rows = master.shape[0]
-    order = sorted(range(1, outer), key=lambda k: abs(2 * k - outer)) + [0]
+    order = sorted(range(1, outer), key=lambda k: (abs(2 * k - outer), -k)) + [0]
+
+    def across(m):
+        at = a
+        for bit in (1 << e for e in range(outer.bit_length())):
+            if m & bit:
+                at = at + bit - 2 * bit * lax.rem(lax.div(a, bit), 2)
+        return at
+
 
     barrier = pltpu.get_barrier_semaphore()
     for j in range(1, inner):
@@ -113,7 +121,7 @@
     shard = rows * LANES
 
     def piece_of(k):
-        first = lax.rem(a + k, outer) * inner
+        first = across(k) * inner
         return pl.ds(pl.multiple_of(first * shard, shard), inner * shard)
 
     pieces = [pltpu.make_async_copy(local_grad.at[0, :, piece_of(k)], raw.at[:, piece_of(k)], raw_sem.at[k]) for k in range(outer)]
@@ -125,7 +133,7 @@
     def widen(k):
         pieces[k].wait()
         for i in range(inner):
-            block = lax.rem(a + k, outer) * inner + i
+            block = across(k) * inner + i
             line = raw[:, pl.ds(pl.multiple_of(block * shard, shard), shard)]
             grad[block] = line.astype(jnp.float32).reshape(rows, LANES)
 
@@ -138,7 +146,7 @@
 
     def near_copy(j, k, h):
         to = a * inner + lax.rem(b + j, inner)
-        block = lax.rem(a + k, outer) * inner + lax.rem(b + j, inner)
+        block = across(k) * inner + lax.rem(b + j, inner)
         sems = near_send.at[j - 1, k, h], near_recv.at[j - 1, k, h]
         return remote(grad.at[block, cuts[h]], near.at[j - 1, k, cuts[h]], *sems, dp=to)
 
@@ -173,12 +181,12 @@
             pl.semaphore_wait(down_sem.at[r], 1)
 
     def far_copy(k, h):
-        to = lax.rem(a + k, outer) * inner + b
+        to = across(k) * inner + b
         sems = far_send.at[k - 1, h], far_recv.at[k - 1, h]
         return remote(partial.at[k - 1, cuts[h]], far.at[k - 1, cuts[h]], *sems, dp=to)
 
     def level_one(k, h):
-        acc = grad[lax.rem(a + k, outer) * inner + b, cuts[h]]
+        acc = grad[across(k) * inner + b, cuts[h]]
         for j in range(1, inner):
             near_copy(j, k, h).wait_recv()
             acc = acc + near[j - 1, k, cuts[h]]

time: 21.8 us -> 21.8 us (level)
  no operation moved by 1% of the time
where the time goes in v3:
time: 21.8 us; the launch traced here: 21.7 us
  Pallas kernels  21 us (96%)
  between operations  0.64 us (3%)
    pallas_call x1, Pallas kernels, on_device(): pl.pallas_call(functools.partial(kernel, n_pair, n_dp), out_shape=[vmem((...  20.3 us
    pallas_call x1, Pallas kernels, on_device(): pl.pallas_call(put_out, out_shape=[jax.ShapeDtypeStruct((2 * rows, LANES)...  0.77 us

profile of v3, /device:TPU:0, one launch (start us, length us, event | category | flops | bytes accessed | tf_op | source)
XLA Modules:
  0.0 21.7 jit_solution(5762996719348251121)
XLA Ops:
  0.6 20.3 %shard_map.76 = (f32[256,128]{1,0:T(8,128)S(1)}, f32[256,128]{1,0:T(8,128)S(1)}, f32[256,128]{1,0:T(8,128)S(1)}) custom-call(s32[1,4]{1,0:T(1,128)} %partner.1, f32[128,128]{1,0:T(8,128)} %bitcast.18, f32[128,128]{1,0:T(8,128)} %bitcast.19, f32[128,128]{1,0:T(8,128)} %bitcast.20, bf16[1,1,131072]{2,1,0:T(2,128)(2,1)} %local_grad.1), custom_call_target="tpu_custom_call" | custom-call | tf_op jit(solution)/shard_map/pallas_call | solution.py:293
  20.9 0.8 %shard_map.77 = (f32[256,128]{1,0:T(8,128)}, f32[256,128]{1,0:T(8,128)}, f32[256,128]{1,0:T(8,128)}) custom-call(f32[256,128]{1,0:T(8,128)S(1)} %get-tuple-element.9.in_w, f32[256,128]{1,0:T(8,128)S(1)} %get-tuple-element.10.in_m, f32[256,128]{1,0:T(8,128)S(1)} %get-tuple-element.11.in_v), custom_call_target="tpu_custom_call" | custom-call | tf_op jit(solution)/shard_map/pallas_call | solution.py:334
